TPU v7x, 32 devices: a whole 2x2x4 slice. The times are simulated.
32 devices in a mesh: group: 2 (over y), seq: 4 (over z), head: 2 (over x), sub: 2 (over core).
Axes of the slice: x: 2, y: 2, z: 4, core: 2. Of those that a mesh axis runs over, the one named last changes fastest.
Arguments:
- queries: bfloat16 [4, 32, 128], P(('group', 'sub'), 'head'), parts along dimension 0, may hold values from -8 to 8
- lengths: int32 [4], P(('group', 'sub')), parts along dimension 0, may hold values from 1 to 192, 256 in all
- k_cache: bfloat16 [65536, 8, 128], P(('group', 'seq', 'sub'), 'head'), parts along dimension 0, may hold values from -12 to 12
- v_cache: bfloat16 [65536, 8, 128], P(('group', 'seq', 'sub'), 'head'), parts along dimension 0, may hold values from -6 to 6
Outputs:
- attended: bfloat16 [4, 32, 128], P('group', ('head', 'sub')), parts along dimension 0
There are 2 independent parts, one for each index of `group`. A program takes and returns all parts, laid end to end along the dimension named above; each array names one. Nothing has to cross between parts.
Inputs may be any that keep to these rules, and one draw needn't show every extreme that they name: The lengths sum to exactly 256, and some request has exactly 192 pages.
All inputs are finite; a program needn't handle non-finite values. No bound on the sum of `lengths` on one device may be relied on, other than what follows from the above.
Results may differ from a plain program's by a relative error of at most 0.0044.
Values may be sent and summed in bfloat16 or wider, within the bound.
A program may use at most 64 MiB of HBM per device.

v0:
```python
import jax
import jax.numpy as jnp
from jax import lax
from jax.sharding import PartitionSpec as P

PAGE = 128


lowest_score = -1e30


def combined_all(x, axis, combine):
    everything = jax.tree.map(lambda part: lax.all_gather(part, axis), x)
    leading = jax.tree.map(lambda part: part[0], everything)

    def turn(k, so_far):
        return combine(so_far, jax.tree.map(lambda part: part[k], everything))

    return lax.fori_loop(1, lax.axis_size(axis), turn, leading)


def joined(first, second):
    highest = jnp.maximum(first[0], second[0])
    lift_first = jnp.exp(first[0] - highest)
    lift_second = jnp.exp(second[0] - highest)
    return (
        highest,
        lift_first * first[1] + lift_second * second[1],
        lift_first[..., None] * first[2] + lift_second[..., None] * second[2],
    )


def shards(queries, lengths, k_cache, v_cache):
    tokens_local = k_cache.shape[0]
    key_heads = k_cache.shape[1]
    head_width = k_cache.shape[2]
    query_heads = queries.shape[1]
    group_size = query_heads // key_heads
    pages_local = tokens_local // PAGE
    every_query = lax.all_gather(queries, "sub", axis=0, tiled=True)
    request_count = every_query.shape[0]
    counts = lax.all_gather(lengths, "sub", axis=0, tiled=True)
    starts = jnp.cumsum(counts) - counts
    position = lax.axis_index(("seq", "sub"))
    page_ids = position * pages_local + jnp.arange(pages_local, dtype=jnp.int32)
    owner = jnp.sum((starts[None, :] <= page_ids[:, None]).astype(jnp.int32), axis=1) - 1
    page_query = jnp.take(every_query, owner, axis=0).reshape(
        pages_local, key_heads, group_size, head_width
    )
    key_pages = k_cache.reshape(pages_local, PAGE, key_heads, head_width)
    value_pages = v_cache.reshape(pages_local, PAGE, key_heads, head_width)
    scores = jnp.einsum(
        "pskd,pkgd->pkgs", key_pages, page_query, preferred_element_type=jnp.float32
    ) * float(head_width) ** (-0.5)
    page_max = jnp.max(scores, axis=3)
    weights = jnp.exp(scores - page_max[..., None])
    page_sum = jnp.sum(weights, axis=3)
    page_out = jnp.einsum(
        "pkgs,pskd->pkgd",
        weights.astype(jnp.bfloat16),
        value_pages,
        preferred_element_type=jnp.float32,
    )
    member = owner[:, None] == jnp.arange(request_count, dtype=jnp.int32)[None, :]
    local_max = jnp.max(
        jnp.where(member[:, :, None, None], page_max[:, None], lowest_score), axis=0
    )
    rescale = jnp.exp(page_max - jnp.take(local_max, owner, axis=0))
    member_float = member.astype(jnp.float32)
    dense_sum = jnp.einsum(
        "pr,pkg->rkg", member_float, rescale * page_sum, precision=lax.Precision.HIGHEST
    ).reshape(request_count, query_heads)
    dense_out = jnp.einsum(
        "pr,pkgd->rkgd",
        member_float,
        rescale[..., None] * page_out,
        precision=lax.Precision.HIGHEST,
    ).reshape(request_count, query_heads, head_width)
    dense_max = local_max.reshape(request_count, query_heads)
    own_heads = query_heads // lax.axis_size("sub")
    head_start = lax.axis_index("sub") * own_heads
    merged = combined_all((dense_max, dense_sum, dense_out), ("seq", "sub"), joined)
    total_sum = merged[1]
    total_out = merged[2]
    denominator = lax.dynamic_slice_in_dim(total_sum, head_start, own_heads, 1)
    summed = lax.dynamic_slice_in_dim(total_out, head_start, own_heads, 1)
    return (summed / denominator[..., None]).astype(jnp.bfloat16)


def solution(mesh):
    return jax.shard_map(
        shards,
        mesh=mesh,
        in_specs=(
            P(("group", "sub"), "head", None),
            P(("group", "sub")),
            P(("group", "seq", "sub"), "head", None),
            P(("group", "seq", "sub"), "head", None),
        ),
        out_specs=P("group", ("head", "sub"), None),
        check_vma=False,
    )
```

profile of v0, /device:TPU:0, one launch (start us, length us, event | category | flops | bytes accessed | tf_op | source)
XLA Modules:
  0.0 55.2 jit_solution(16053141113954423485)
XLA Ops:
  0.0 2.1 %all_gather.16 = bf16[2,16,128]{2,1,0:T(8,128)(2,1)S(1)} all-gather(bf16[1,16,128]{2,1,0:T(8,128)(2,1)} %param.6), channel_id=1, replica_groups=mesh['group'=2,'seq'=4,'head'=2,'sub'=2] {'sub'}, dimensions={0}, use_global_device_ids=true | all-gather | bytes 12288 | tf_op jit(solution)/shard_map/all_gather | solution.py:40
  2.7 1.3 %dynamic-slice = u32[1]{0:T(128)} dynamic-slice(u32[32]{0:T(128)} %constant.102, u32[]{:T(128)S(6)} %add.121), dynamic_slice_sizes={1} | dynamic-slice | bytes 12
  4.1 0.8 %dynamic-update-slice = s32[2]{0:T(128)S(1)} dynamic-update-slice(s32[2]{0:T(128)S(1)} %broadcast.79, s32[1]{0:T(128)S(6)} %copy.52, u32[]{:T(128)} %bitcast.3) | dynamic-update-slice | bytes 12
  4.9 1.8 %all-reduce = s32[2]{0:T(128)S(1)} all-reduce(s32[2]{0:T(128)S(1)} %dynamic-update-slice), channel_id=1, replica_groups=mesh['group'=2,'seq'=4,'head'=2,'sub'=2] {'sub'}, use_global_device_ids=true, to_apply=%add | all-reduce | flops 2 | bytes 16
  6.7 0.2 reduce-window.9
  6.9 0.1 fusion.26
  7.0 0.6 %gather_fusion = bf16[32,16,128]{2,1,0:T(8,128)(2,1)S(1)} fusion(bf16[2,16,128]{2,1,0:T(8,128)(2,1)S(1)} %all_gather.16, s32[1024]{0:T(1024)S(1)} %pad_clamp_fusion), kind=kCustom, calls=%fused_computation | custom fusion | bytes 262272 | tf_op jit(solution)/shard_map/jit(_take)/gather | solution.py:47
  7.6 4.6 %fusion.31 = (f32[32,4,4]{2,1,0:T(4,128)S(1)}, f32[32,4,4,128]{3,2,1,0:T(4,128)S(1)}) fusion(bf16[32,128,4,128]{3,2,1,0:T(4,128)(2,1)} %bitcast.49, bf16[32,4,4,128]{3,2,1,0:T(4,128)(2,1)S(1)} %bitcast.47, pred[32]{0:T(512)(128)(4,1)S(1)} %compare_and_fusion), kind=kOutput, calls=%fused_computation.50 | convolution fusion | flops 16973312 | bytes 4589600 | tf_op jit(solution)/shard_map/pskd,pkgd->pkgs/dot_general | solution.py:52
  12.2 0.1 copy.18
  12.3 0.1 select_reduce_fusion
  12.4 0.1 all_gather_reshape.9
  12.5 13.3 %all_gather.17 = f32[8,2,16]{2,1,0:T(2,128)S(1)} all-gather(f32[1,2,16]{2,1,0:T(2,128)S(1)} %all_gather_reshape.9), channel_id=1, replica_groups=mesh['group'=2,'seq'=4,'head'=2,'sub'=2] {'seq','sub'}, dimensions={0}, use_global_device_ids=true | all-gather | bytes 1152 | tf_op jit(solution)/shard_map/all_gather | solution.py:13
  25.8 0.4 fusion.16
  26.3 0.6 %gather_fusion.1 = f32[32,4,4]{2,1,0:T(4,128)S(1)} fusion(f32[2,4,4]{2,1,0:T(4,128)S(1)} %select_reduce_fusion, s32[1024]{0:T(1024)S(1)} %pad_clamp_fusion), kind=kCustom, calls=%fused_computation.1 | custom fusion | bytes 4224 | tf_op jit(solution)/shard_map/jit(_take)/gather | solution.py:68
  26.9 0.1 fusion.30
  27.0 0.1 fusion.21
  27.1 0.1 all_gather_reshape.10
  27.2 8.7 %all_gather.18 = f32[8,2,16]{2,1,0:T(2,128)S(1)} all-gather(f32[1,2,16]{2,1,0:T(2,128)S(1)} %all_gather_reshape.10), channel_id=1, replica_groups=mesh['group'=2,'seq'=4,'head'=2,'sub'=2] {'seq','sub'}, dimensions={0}, use_global_device_ids=true | all-gather | bytes 1152 | tf_op jit(solution)/shard_map/all_gather | solution.py:13
  36.0 3.5 %fusion.10 = f32[32,4,4,128]{3,2,1,0:T(4,128)S(1)} fusion(bf16[32,128,4,128]{3,2,1,0:T(4,128)(2,1)} %bitcast.50, f32[32,4,4,128]{3,2,1,0:T(4,128)S(1)} %get-tuple-element.205, f32[32,4,4]{2,1,0:T(4,128)S(1)} %get-tuple-element.203, f32[32,4,4]{2,1,0:T(4,128)S(1)} %get-tuple-element.204), kind=kOutput, calls=%fused_computation.16 | convolution fusion | flops 16973824 | bytes 4722688 | tf_op jit(solution)/shard_map/pkgs,pskd->pkgd/dot_general | solution.py:58
  39.4 0.3 fusion.13
  39.7 14.0 %all_gather.19 = f32[8,2,16,128]{3,2,1,0:T(8,128)S(1)} all-gather(f32[1,2,16,128]{3,2,1,0:T(8,128)S(1)} %copy.23), channel_id=1, replica_groups=mesh['group'=2,'seq'=4,'head'=2,'sub'=2] {'seq','sub'}, dimensions={0}, use_global_device_ids=true | all-gather | bytes 147456 | tf_op jit(solution)/shard_map/all_gather | solution.py:13
  53.7 0.7 %while.19 = (s32[]{:T(128)}, f32[2,16]{1,0:T(2,128)S(1)}, f32[2,16]{1,0:T(2,128)S(1)}, f32[2,16,128]{2,1,0:T(8,128)S(1)}, f32[8,2,16]{2,1,0:T(2,128)S(1)}, /*ind...) while((s32[]{:T(128)}, f32[2,16]{1,0:T(2,128)S(1)}, ...), condition=%wide.region_6.7_spmd, body=%wide.region_5.6_spmd.sunk | while | flops 12485 | bytes 50583 | solution.py:19
  53.7 0.1 fusion.35
  53.8 0.1 fusion.35
  53.9 0.1 fusion.35
  54.0 0.1 fusion.35
  54.1 0.1 fusion.35
  54.2 0.1 fusion.35
  54.3 0.1 fusion.35
  54.4 0.1 constant_dynamic-slice_fusion.1
  54.5 0.7 %divide_convert_fusion = bf16[2,8,128]{2,1,0:T(8,128)(2,1)} fusion(f32[2,16,128]{2,1,0:T(8,128)S(1)} %get-tuple-element.182, s32[]{:T(128)S(6)} %select_n.56, f32[2,8]{1,0:T(2,128)S(1)} %constant_dynamic-slice_fusion.1), kind=kLoop, calls=%fused_computation.31 | loop fusion | flops 4096 | bytes 12356 | tf_op jit(solution)/shard_map/convert_element_type | solution.py:87
  (20 shorter events, 0.2 us)
where the time goes:
time: 55.4 us; the launch traced here: 55.2 us
  blocking collectives  40 us (72%)
  matrix products  8.48 us (15%)
  local copies, waits for them, and re-layouts  3.68 us (7%)
  other arithmetic  2.31 us (4%)
  between operations  0.72 us (1%)
    all_gather x3, blocking collectives, combined_all(): everything = jax.tree.map(lambda part: lax.all_gather(part, axis), x)  36 us
    dot_general x1, matrix products, shards(): jnp.einsum('pskd,pkgd->pkgs', key_pages, page_query, preferred_element_ty...  4.6 us
    dot_general x1, matrix products, shards(): jnp.einsum('pkgs,pskd->pkgd', weights.astype(jnp.bfloat16), value_pages,...  3.46 us
    unnamed x3, local copies, waits for them, and re-layouts  2.12 us
    all_gather x1, blocking collectives, shards(): every_query = lax.all_gather(queries, 'sub', axis=0, tiled=True)  2.08 us
    unnamed x1, blocking collectives  1.83 us

commit v1 on v0

v1 whole, which is shorter than its diff:
```python
import functools
import math

import jax
import jax.numpy as jnp
from jax import lax
from jax.experimental import pallas as pl
from jax.experimental.pallas import tpu as pltpu
from jax.sharding import PartitionSpec as P

PAGE = 128
MESH = pl.DeviceIdType.MESH
LOWEST = -1e30


def kernel(
    n, subs, pages, unroll, key_heads, own_requests, group_size, head_width,
    q_in, len_in, k_in, v_in, out_ref,
    q_all, len_all, k_buf, v_buf, s_buf, m_buf, send, recv,
    q_sems, len_sems, k_sems, v_sems, send_sems, recv_sems,
):
    requests = own_requests * subs
    query_heads = key_heads * group_size
    own_heads = query_heads // subs
    rows = PAGE * key_heads
    steps = pages // unroll
    span = rows * unroll
    sub = lax.axis_index("sub")
    me = lax.axis_index("seq") * subs + sub

    def k_copy(i):
        at = pl.ds(pl.multiple_of(i * span, span), span)
        return pltpu.make_async_copy(k_in.at[at], k_buf.at[at], k_sems.at[i])

    def v_copy(i):
        at = pl.ds(pl.multiple_of(i * span, span), span)
        return pltpu.make_async_copy(v_in.at[at], v_buf.at[at], v_sems.at[i])

    def peer(k):
        other = lax.rem(me + k, n)
        return other // subs, lax.rem(other, subs)

    barrier = pltpu.get_barrier_semaphore()
    for k in range(1, n):
        other_seq, other_sub = peer(k)
        pl.semaphore_signal(
            barrier, inc=1, device_id={"seq": other_seq, "sub": other_sub}, device_id_type=MESH
        )
    own_q = pltpu.make_async_copy(q_in, q_all.at[sub], q_sems.at[0])
    own_q.start()
    own_len = pltpu.make_async_copy(len_in, len_all.at[sub], len_sems.at[0])
    own_len.start()
    for i in range(steps):
        k_copy(i).start()
    for i in range(steps):
        v_copy(i).start()
    pl.semaphore_wait(barrier, n - 1)

    copies = []
    for k in range(1, subs):
        other = {"sub": lax.rem(sub + k, subs)}
        copies.append(pltpu.make_async_remote_copy(
            src_ref=q_all.at[sub], dst_ref=q_all.at[sub], send_sem=q_sems.at[2 * k - 1],
            recv_sem=q_sems.at[2 * k], device_id=other, device_id_type=MESH,
        ))
        copies.append(pltpu.make_async_remote_copy(
            src_ref=len_all.at[sub], dst_ref=len_all.at[sub], send_sem=len_sems.at[2 * k - 1],
            recv_sem=len_sems.at[2 * k], device_id=other, device_id_type=MESH,
        ))
    own_q.wait()
    own_len.wait()
    for copy in copies:
        copy.start()
    for copy in copies:
        copy.wait()

    starts, total = [], jnp.int32(0)
    for r in range(requests):
        starts.append(total)
        total = total + len_all[r // own_requests, 0, r % own_requests]
    first_page = me * pages

    def owner_of(page):
        owner = jnp.int32(-1)
        for start in starts:
            owner = owner + (start <= first_page + page).astype(jnp.int32)
        return owner

    lane = lax.broadcasted_iota(jnp.int32, (query_heads, rows), 1)
    row = lax.broadcasted_iota(jnp.int32, (query_heads, rows), 0)
    matching = lax.rem(lane, key_heads) == row // group_size
    contract_last = (((1,), (1,)), ((), ()))

    def scores(i, highest):
        k_copy(i).wait()
        for j in range(unroll):
            page = i * unroll + j
            owner = owner_of(page)
            query = q_all[owner // own_requests, lax.rem(owner, own_requests)]
            at = pl.ds(pl.multiple_of(page * rows, rows), rows)
            score = lax.dot_general(
                query, k_buf[at, :], contract_last, preferred_element_type=jnp.float32
            )
            score = jnp.where(matching, score, LOWEST)
            s_buf[page] = score
            top = score[:, :head_width]
            for c in range(1, rows // head_width):
                top = jnp.maximum(top, score[:, c * head_width:(c + 1) * head_width])
            highest = tuple(
                jnp.maximum(highest[r], jnp.where(owner == r, top, LOWEST)) for r in range(requests)
            )
        return highest

    lowest = jnp.full((query_heads, head_width), LOWEST, jnp.float32)
    highest = lax.fori_loop(0, steps, scores, (lowest,) * requests)
    local_max = []
    for r in range(requests):
        top = jnp.broadcast_to(jnp.max(highest[r], axis=1, keepdims=True), lowest.shape)
        m_buf[r] = top
        local_max.append(top)

    factor = float(head_width) ** -0.5 * math.log2(math.e)
    repeat = rows // head_width

    def values(i, so_far):
        v_copy(i).wait()
        sums, outs = so_far
        for j in range(unroll):
            page = i * unroll + j
            owner = owner_of(page)
            top = m_buf[owner]
            at = pl.ds(pl.multiple_of(page * rows, rows), rows)
            pieces = [
                jnp.exp2((s_buf[page, :, c * head_width:(c + 1) * head_width] - top) * factor)
                for c in range(repeat)
            ]
            page_sum = pieces[0]
            for piece in pieces[1:]:
                page_sum = page_sum + piece
            weights = jnp.concatenate([piece.astype(jnp.bfloat16) for piece in pieces], axis=1)
            page_out = jnp.dot(weights, v_buf[at, :], preferred_element_type=jnp.float32)
            sums = tuple(sums[r] + jnp.where(owner == r, page_sum, 0.0) for r in range(requests))
            outs = tuple(outs[r] + jnp.where(owner == r, page_out, 0.0) for r in range(requests))
        return sums, outs

    zero = jnp.zeros((query_heads, head_width), jnp.float32)
    sums, outs = lax.fori_loop(0, steps, values, ((zero,) * requests, (zero,) * requests))

    low_lanes = lax.broadcasted_iota(jnp.int32, zero.shape, 1) < head_width // 2
    for r in range(requests):
        local_sum = jnp.broadcast_to(jnp.sum(sums[r], axis=1, keepdims=True), zero.shape)
        stats = jnp.where(low_lanes, local_max[r], local_sum)
        for half in range(subs):
            part = slice(half * own_heads, (half + 1) * own_heads)
            send[half, r] = outs[r][part]
            send[half, requests + r] = stats[part]

    copies = []
    for k in range(1, n):
        other_seq, other_sub = peer(k)
        copies.append(pltpu.make_async_remote_copy(
            src_ref=send.at[other_sub], dst_ref=recv.at[k - 1], send_sem=send_sems.at[k - 1],
            recv_sem=recv_sems.at[k - 1], device_id={"seq": other_seq, "sub": other_sub},
            device_id_type=MESH,
        ))
        copies[-1].start()
    for copy in copies:
        copy.wait_recv()

    half_width = head_width // 2
    for r in range(requests):
        parts = [(send[sub, requests + r], send[sub, r])]
        for k in range(n - 1):
            parts.append((recv[k, requests + r], recv[k, r]))
        top = parts[0][0]
        for stats, _ in parts[1:]:
            top = jnp.maximum(top, stats)
        top = top[:, :1]
        denominator = jnp.zeros((own_heads, 1), jnp.float32)
        numerator = jnp.zeros((own_heads, head_width), jnp.float32)
        for stats, out in parts:
            lift = jnp.exp2((stats[:, :1] - top) * factor)
            denominator = denominator + lift * stats[:, half_width:half_width + 1]
            numerator = numerator + lift * out
        out_ref[r] = (numerator / denominator).astype(out_ref.dtype)
    for copy in copies:
        copy.wait_send()


def shards(seqs, subs, queries, lengths, k_cache, v_cache):
    tokens, key_heads, head_width = k_cache.shape
    own_requests, query_heads, _ = queries.shape
    group_size = query_heads // key_heads
    requests = own_requests * subs
    pages = tokens // PAGE
    unroll = math.gcd(4, pages)
    steps = pages // unroll
    rows = PAGE * key_heads
    n = seqs * subs
    own_heads = query_heads // subs
    anywhere = pl.BlockSpec(memory_space=pltpu.HBM)
    sems = pltpu.SemaphoreType.DMA
    return pl.pallas_call(
        functools.partial(
            kernel, n, subs, pages, unroll, key_heads, own_requests, group_size, head_width
        ),
        out_shape=jax.ShapeDtypeStruct((requests, own_heads, head_width), jnp.bfloat16),
        in_specs=[anywhere] * 4,
        out_specs=pl.BlockSpec(memory_space=pltpu.VMEM),
        scratch_shapes=[
            pltpu.VMEM((subs, own_requests, query_heads, head_width), jnp.bfloat16),
            pltpu.SMEM((subs, 1, own_requests), jnp.int32),
            pltpu.VMEM((tokens * key_heads, head_width), jnp.bfloat16),
            pltpu.VMEM((tokens * key_heads, head_width), jnp.bfloat16),
            pltpu.VMEM((pages, query_heads, rows), jnp.float32),
            pltpu.VMEM((requests, query_heads, head_width), jnp.float32),
            pltpu.VMEM((subs, 2 * requests, own_heads, head_width), jnp.float32),
            pltpu.VMEM((n - 1, 2 * requests, own_heads, head_width), jnp.float32),
            sems((2 * subs - 1,)),
            sems((2 * subs - 1,)),
            sems((steps,)),
            sems((steps,)),
            sems((n - 1,)),
            sems((n - 1,)),
        ],
        compiler_params=pltpu.CompilerParams(
            collective_id=0, has_side_effects=True, vmem_limit_bytes=63 * 1024 * 1024
        ),
    )(
        queries,
        lengths.reshape(1, own_requests),
        k_cache.reshape(tokens * key_heads, head_width),
        v_cache.reshape(tokens * key_heads, head_width),
    )


def solution(mesh):
    return jax.shard_map(
        functools.partial(shards, mesh.shape["seq"], mesh.shape["sub"]),
        mesh=mesh,
        in_specs=(
            P(("group", "sub"), "head", None),
            P(("group", "sub")),
            P(("group", "seq", "sub"), "head", None),
            P(("group", "seq", "sub"), "head", None),
        ),
        out_specs=P("group", ("head", "sub"), None),
        check_vma=False,
    )
```

time: 55.4 us -> 18.2 us (0.33)
  blocking collectives: 40 us -> 0 us
  Pallas kernels: 0 us -> 16.1 us
  matrix products: 8.48 us -> 0 us
  local copies, waits for them, and re-layouts: 3.68 us -> 1.28 us
  other arithmetic: 2.31 us -> 0 us
    all_gather x4 -> x0, blocking collectives: 38.1 us -> none  [the longest x3 36 us: combined_all(): everything = jax.tree.map(lambda part: lax.all_gather(part, axis), x)]
    pallas_call x0 -> x1, Pallas kernels: none -> 16.1 us  [shards(): pl.pallas_call(functools.partial(kernel, n, subs, pages, unroll, key_head...]
    dot_general x4 -> x0, matrix products: 8.48 us -> none  [the longest x1 4.6 us: shards(): jnp.einsum('pskd,pkgd->pkgs', key_pages, page_query, preferred_element_ty...]
    unnamed x1 -> x0, blocking collectives: 1.83 us -> none
    gather x2 -> x0, local copies, waits for them, and re-layouts: 1.2 us -> none  [the longest x1 0.61 us: shards(): rescale = jnp.exp(page_max - jnp.take(local_max, owner, axis=0))]
    unnamed x3 -> x1, local copies, waits for them, and re-layouts: 2.12 us -> 1.28 us
    add x15 -> x0, other arithmetic: 0.69 us -> none  [the longest x7 0.55 us: joined(): lift_first[..., None] * first[2] + lift_second[..., None] * second[2]]
    convert_element_type x1 -> x0, other arithmetic: 0.68 us -> none  [shards(): return (summed / denominator[..., None]).astype(jnp.bfloat16)]
where the time goes in v1:
time: 18.2 us; the launch traced here: 18.1 us
  Pallas kernels  16.1 us (88%)
  local copies, waits for them, and re-layouts  1.28 us (7%)
  between operations  0.66 us (4%)
    pallas_call x1, Pallas kernels, shards(): pl.pallas_call(functools.partial(kernel, n, subs, pages, unroll, key_head...  16.1 us
    unnamed x1, local copies, waits for them, and re-layouts  1.28 us

profile of v1, /device:TPU:0, one launch (start us, length us, event | category | flops | bytes accessed | tf_op | source)
XLA Modules:
  0.0 18.1 jit_solution(257992023567676157)
XLA Ops:
  0.7 16.1 %shard_map.46 = bf16[2,8,128]{2,1,0:T(8,128)(2,1)} custom-call(bf16[1,16,128]{2,1,0:T(8,128)(2,1)} %q_in.1, s32[1,1]{1,0:T(1,128)} %bitcast.3.len_in, bf16[16384,128]{1,0:T(8,128)(2,1)} %bitcast.4, bf16[16384,128]{1,0:T(8,128)(2,1)} %bitcast.5), custom_call_target="tpu_custom_call" | custom-call | tf_op jit(solution)/shard_map/pallas_call | solution.py:203
  16.8 1.3 %copy.7 = bf16[2,8,128]{2,1,0:T(8,128)(2,1)} copy(bf16[2,8,128]{2,1,0:T(8,128)(2,1)} %shard_map.46) | data formatting | bytes 8192

commit v2 on v1

--- a/solution.py
+++ b/solution.py
@@ -52,7 +52,6 @@
     own_len.start()
     for i in range(steps):
         k_copy(i).start()
-    for i in range(steps):
         v_copy(i).start()
     pl.semaphore_wait(barrier, n - 1)
 
@@ -91,60 +90,65 @@
     matching = lax.rem(lane, key_heads) == row // group_size
     contract_last = (((1,), (1,)), ((), ()))
 
-    def scores(i, highest):
+    factor = float(head_width) ** -0.5 * math.log2(math.e)
+    repeat = rows // head_width
+    lowest = jnp.full((query_heads, head_width), LOWEST, jnp.float32)
+
+    def attend(i, highest):
         k_copy(i).wait()
+        owners, all_scores = [], []
         for j in range(unroll):
             page = i * unroll + j
             owner = owner_of(page)
+            owners.append(owner)
             query = q_all[owner // own_requests, lax.rem(owner, own_requests)]
             at = pl.ds(pl.multiple_of(page * rows, rows), rows)
             score = lax.dot_general(
                 query, k_buf[at, :], contract_last, preferred_element_type=jnp.float32
             )
-            score = jnp.where(matching, score, LOWEST)
-            s_buf[page] = score
+            all_scores.append(jnp.where(matching, score, LOWEST))
+        v_copy(i).wait()
+        for j in range(unroll):
+            page, owner, score = i * unroll + j, owners[j], all_scores[j]
             top = score[:, :head_width]
-            for c in range(1, rows // head_width):
+            for c in range(1, repeat):
                 top = jnp.maximum(top, score[:, c * head_width:(c + 1) * head_width])
-            highest = tuple(
-                jnp.maximum(highest[r], jnp.where(owner == r, top, LOWEST)) for r in range(requests)
-            )
-        return highest
-
-    lowest = jnp.full((query_heads, head_width), LOWEST, jnp.float32)
-    highest = lax.fori_loop(0, steps, scores, (lowest,) * requests)
-    local_max = []
-    for r in range(requests):
-        top = jnp.broadcast_to(jnp.max(highest[r], axis=1, keepdims=True), lowest.shape)
-        m_buf[r] = top
-        local_max.append(top)
-
-    factor = float(head_width) ** -0.5 * math.log2(math.e)
-    repeat = rows // head_width
-
-    def values(i, so_far):
-        v_copy(i).wait()
-        sums, outs = so_far
-        for j in range(unroll):
-            page = i * unroll + j
-            owner = owner_of(page)
-            top = m_buf[owner]
-            at = pl.ds(pl.multiple_of(page * rows, rows), rows)
+            top = jnp.broadcast_to(jnp.max(top, axis=1, keepdims=True), lowest.shape)
             pieces = [
-                jnp.exp2((s_buf[page, :, c * head_width:(c + 1) * head_width] - top) * factor)
+                jnp.exp2((score[:, c * head_width:(c + 1) * head_width] - top) * factor)
                 for c in range(repeat)
             ]
             page_sum = pieces[0]
             for piece in pieces[1:]:
                 page_sum = page_sum + piece
             weights = jnp.concatenate([piece.astype(jnp.bfloat16) for piece in pieces], axis=1)
-            page_out = jnp.dot(weights, v_buf[at, :], preferred_element_type=jnp.float32)
+            at = pl.ds(pl.multiple_of(page * rows, rows), rows)
+            s_buf[page, 0] = top
+            s_buf[page, 1] = page_sum
+            s_buf[page, 2] = jnp.dot(weights, v_buf[at, :], preferred_element_type=jnp.float32)
+            highest = tuple(
+                jnp.maximum(highest[r], jnp.where(owner == r, top, LOWEST)) for r in range(requests)
+            )
+        return highest
+
+    local_max = lax.fori_loop(0, steps, attend, (lowest,) * requests)
+    for r in range(requests):
+        m_buf[r] = local_max[r]
+
+    def combine(i, so_far):
+        sums, outs = so_far
+        for j in range(unroll):
+            page = i * unroll + j
+            owner = owner_of(page)
+            lift = jnp.exp2((s_buf[page, 0] - m_buf[owner]) * factor)
+            page_sum = lift * s_buf[page, 1]
+            page_out = lift * s_buf[page, 2]
             sums = tuple(sums[r] + jnp.where(owner == r, page_sum, 0.0) for r in range(requests))
             outs = tuple(outs[r] + jnp.where(owner == r, page_out, 0.0) for r in range(requests))
         return sums, outs
 
     zero = jnp.zeros((query_heads, head_width), jnp.float32)
-    sums, outs = lax.fori_loop(0, steps, values, ((zero,) * requests, (zero,) * requests))
+    sums, outs = lax.fori_loop(0, steps, combine, ((zero,) * requests, (zero,) * requests))
 
     low_lanes = lax.broadcasted_iota(jnp.int32, zero.shape, 1) < head_width // 2
     for r in range(requests):
@@ -193,7 +197,7 @@
     group_size = query_heads // key_heads
     requests = own_requests * subs
     pages = tokens // PAGE
-    unroll = math.gcd(4, pages)
+    unroll = math.gcd(8, pages)
     steps = pages // unroll
     rows = PAGE * key_heads
     n = seqs * subs
@@ -212,7 +216,7 @@
             pltpu.SMEM((subs, 1, own_requests), jnp.int32),
             pltpu.VMEM((tokens * key_heads, head_width), jnp.bfloat16),
             pltpu.VMEM((tokens * key_heads, head_width), jnp.bfloat16),
-            pltpu.VMEM((pages, query_heads, rows), jnp.float32),
+            pltpu.VMEM((pages, 3, query_heads, head_width), jnp.float32),
             pltpu.VMEM((requests, query_heads, head_width), jnp.float32),
             pltpu.VMEM((subs, 2 * requests, own_heads, head_width), jnp.float32),
             pltpu.VMEM((n - 1, 2 * requests, own_heads, head_width), jnp.float32),

time: 18.2 us -> 17.5 us (0.962)
  Pallas kernels: 16.1 us -> 15.4 us
    pallas_call x1, Pallas kernels: 16.1 us -> 15.4 us  [shards(): pl.pallas_call(functools.partial(kernel, n, subs, pages, unroll, key_head...]
where the time goes in v2:
time: 17.5 us; the launch traced here: 17.3 us
  Pallas kernels  15.4 us (88%)
  local copies, waits for them, and re-layouts  1.28 us (7%)
  between operations  0.66 us (4%)
    pallas_call x1, Pallas kernels, shards(): pl.pallas_call(functools.partial(kernel, n, subs, pages, unroll, key_head...  15.4 us
    unnamed x1, local copies, waits for them, and re-layouts  1.28 us

profile of v2, /device:TPU:0, one launch (start us, length us, event | category | flops | bytes accessed | tf_op | source)
XLA Modules:
  0.0 17.3 jit_solution(12156785884407863934)
XLA Ops:
  0.7 15.4 %shard_map.46 = bf16[2,8,128]{2,1,0:T(8,128)(2,1)} custom-call(bf16[1,16,128]{2,1,0:T(8,128)(2,1)} %q_in.1, s32[1,1]{1,0:T(1,128)} %bitcast.3.len_in, bf16[16384,128]{1,0:T(8,128)(2,1)} %bitcast.4, bf16[16384,128]{1,0:T(8,128)(2,1)} %bitcast.5), custom_call_target="tpu_custom_call" | custom-call | tf_op jit(solution)/shard_map/pallas_call | solution.py:207
  16.0 1.3 %copy.7 = bf16[2,8,128]{2,1,0:T(8,128)(2,1)} copy(bf16[2,8,128]{2,1,0:T(8,128)(2,1)} %shard_map.46) | data formatting | bytes 8192

commit v3 on v2

--- a/solution.py
+++ b/solution.py
@@ -16,8 +16,9 @@
 def kernel(
     n, subs, pages, unroll, key_heads, own_requests, group_size, head_width,
     q_in, len_in, k_in, v_in, out_ref,
-    q_all, len_all, k_buf, v_buf, s_buf, m_buf, send, recv,
+    q_all, len_all, k_buf, v_buf, s_buf, m_buf, send, recv, send_stats, recv_stats,
     q_sems, len_sems, k_sems, v_sems, send_sems, recv_sems,
+    stat_send_sems, stat_recv_sems,
 ):
     requests = own_requests * subs
     query_heads = key_heads * group_size
@@ -150,42 +151,48 @@
     zero = jnp.zeros((query_heads, head_width), jnp.float32)
     sums, outs = lax.fori_loop(0, steps, combine, ((zero,) * requests, (zero,) * requests))
 
-    low_lanes = lax.broadcasted_iota(jnp.int32, zero.shape, 1) < head_width // 2
+    stat_lane = lax.broadcasted_iota(jnp.int32, zero.shape, 1)
+    stats = zero
     for r in range(requests):
         local_sum = jnp.broadcast_to(jnp.sum(sums[r], axis=1, keepdims=True), zero.shape)
-        stats = jnp.where(low_lanes, local_max[r], local_sum)
-        for half in range(subs):
-            part = slice(half * own_heads, (half + 1) * own_heads)
-            send[half, r] = outs[r][part]
-            send[half, requests + r] = stats[part]
+        stats = jnp.where(stat_lane == 2 * r, local_max[r], stats)
+        stats = jnp.where(stat_lane == 2 * r + 1, local_sum, stats)
+    for half in range(subs):
+        part = slice(half * own_heads, (half + 1) * own_heads)
+        send_stats[half] = stats[part]
+        for r in range(requests):
+            send[half, r] = outs[r][part].astype(jnp.bfloat16)
 
     copies = []
     for k in range(1, n):
         other_seq, other_sub = peer(k)
+        other = {"seq": other_seq, "sub": other_sub}
+        copies.append(pltpu.make_async_remote_copy(
+            src_ref=send_stats.at[other_sub], dst_ref=recv_stats.at[k - 1],
+            send_sem=stat_send_sems.at[k - 1], recv_sem=stat_recv_sems.at[k - 1],
+            device_id=other, device_id_type=MESH,
+        ))
+        copies[-1].start()
         copies.append(pltpu.make_async_remote_copy(
             src_ref=send.at[other_sub], dst_ref=recv.at[k - 1], send_sem=send_sems.at[k - 1],
-            recv_sem=recv_sems.at[k - 1], device_id={"seq": other_seq, "sub": other_sub},
-            device_id_type=MESH,
+            recv_sem=recv_sems.at[k - 1], device_id=other, device_id_type=MESH,
         ))
         copies[-1].start()
     for copy in copies:
         copy.wait_recv()
 
-    half_width = head_width // 2
-    for r in range(requests):
-        parts = [(send[sub, requests + r], send[sub, r])]
-        for k in range(n - 1):
-            parts.append((recv[k, requests + r], recv[k, r]))
-        top = parts[0][0]
-        for stats, _ in parts[1:]:
-            top = jnp.maximum(top, stats)
-        top = top[:, :1]
+    all_stats = [send_stats[sub]] + [recv_stats[k] for k in range(n - 1)]
+    top = all_stats[0]
+    for part in all_stats[1:]:
+        top = jnp.maximum(top, part)
+    for r in range(requests):
         denominator = jnp.zeros((own_heads, 1), jnp.float32)
         numerator = jnp.zeros((own_heads, head_width), jnp.float32)
-        for stats, out in parts:
-            lift = jnp.exp2((stats[:, :1] - top) * factor)
-            denominator = denominator + lift * stats[:, half_width:half_width + 1]
-            numerator = numerator + lift * out
+        for k, part in enumerate(all_stats):
+            out = send[sub, r] if k == 0 else recv[k - 1, r]
+            lift = jnp.exp2((part[:, 2 * r:2 * r + 1] - top[:, 2 * r:2 * r + 1]) * factor)
+            denominator = denominator + lift * part[:, 2 * r + 1:2 * r + 2]
+            numerator = numerator + lift * out.astype(jnp.float32)
         out_ref[r] = (numerator / denominator).astype(out_ref.dtype)
     for copy in copies:
         copy.wait_send()
@@ -218,12 +225,16 @@
             pltpu.VMEM((tokens * key_heads, head_width), jnp.bfloat16),
             pltpu.VMEM((pages, 3, query_heads, head_width), jnp.float32),
             pltpu.VMEM((requests, query_heads, head_width), jnp.float32),
-            pltpu.VMEM((subs, 2 * requests, own_heads, head_width), jnp.float32),
-            pltpu.VMEM((n - 1, 2 * requests, own_heads, head_width), jnp.float32),
+            pltpu.VMEM((subs, requests, own_heads, head_width), jnp.bfloat16),
+            pltpu.VMEM((n - 1, requests, own_heads, head_width), jnp.bfloat16),
+            pltpu.VMEM((subs, own_heads, head_width), jnp.float32),
+            pltpu.VMEM((n - 1, own_heads, head_width), jnp.float32),
             sems((2 * subs - 1,)),
             sems((2 * subs - 1,)),
             sems((steps,)),
             sems((steps,)),
+            sems((n - 1,)),
+            sems((n - 1,)),
             sems((n - 1,)),
             sems((n - 1,)),
         ],

time: 17.5 us -> 17.3 us (0.989)
  Pallas kernels: 15.4 us -> 15.2 us
where the time goes in v3:
time: 17.3 us; the launch traced here: 17.1 us
  Pallas kernels  15.2 us (88%)
  local copies, waits for them, and re-layouts  1.28 us (7%)
  between operations  0.66 us (4%)
    pallas_call x1, Pallas kernels, shards(): pl.pallas_call(functools.partial(kernel, n, subs, pages, unroll, key_head...  15.2 us
    unnamed x1, local copies, waits for them, and re-layouts  1.28 us

profile of v3, /device:TPU:0, one launch (start us, length us, event | category | flops | bytes accessed | tf_op | source)
XLA Modules:
  0.0 17.1 jit_solution(11453476256013827437)
XLA Ops:
  0.7 15.2 %shard_map.46 = bf16[2,8,128]{2,1,0:T(8,128)(2,1)} custom-call(bf16[1,16,128]{2,1,0:T(8,128)(2,1)} %q_in.1, s32[1,1]{1,0:T(1,128)} %bitcast.3.len_in, bf16[16384,128]{1,0:T(8,128)(2,1)} %bitcast.4, bf16[16384,128]{1,0:T(8,128)(2,1)} %bitcast.5), custom_call_target="tpu_custom_call" | custom-call | tf_op jit(solution)/shard_map/pallas_call | solution.py:214
  15.9 1.3 %copy.7 = bf16[2,8,128]{2,1,0:T(8,128)(2,1)} copy(bf16[2,8,128]{2,1,0:T(8,128)(2,1)} %shard_map.46) | data formatting | bytes 8192

commit v4 on v2

--- a/solution.py
+++ b/solution.py
@@ -197,7 +197,7 @@
     group_size = query_heads // key_heads
     requests = own_requests * subs
     pages = tokens // PAGE
-    unroll = math.gcd(8, pages)
+    unroll = math.gcd(16, pages)
     steps = pages // unroll
     rows = PAGE * key_heads
     n = seqs * subs

time: 17.5 us -> 16.2 us (0.926)
  Pallas kernels: 15.4 us -> 14.1 us
    pallas_call x1, Pallas kernels: 15.4 us -> 14.1 us  [shards(): pl.pallas_call(functools.partial(kernel, n, subs, pages, unroll, key_head...]
where the time goes in v4:
time: 16.2 us; the launch traced here: 16 us
  Pallas kernels  14.1 us (87%)
  local copies, waits for them, and re-layouts  1.28 us (8%)
  between operations  0.66 us (4%)
    pallas_call x1, Pallas kernels, shards(): pl.pallas_call(functools.partial(kernel, n, subs, pages, unroll, key_head...  14.1 us
    unnamed x1, local copies, waits for them, and re-layouts  1.28 us

profile of v4, /device:TPU:0, one launch (start us, length us, event | category | flops | bytes accessed | tf_op | source)
XLA Modules:
  0.0 16.0 jit_solution(11508327807384911523)
XLA Ops:
  0.7 14.1 %shard_map.46 = bf16[2,8,128]{2,1,0:T(8,128)(2,1)} custom-call(bf16[1,16,128]{2,1,0:T(8,128)(2,1)} %q_in.1, s32[1,1]{1,0:T(1,128)} %bitcast.3.len_in, bf16[16384,128]{1,0:T(8,128)(2,1)} %bitcast.4, bf16[16384,128]{1,0:T(8,128)(2,1)} %bitcast.5), custom_call_target="tpu_custom_call" | custom-call | tf_op jit(solution)/shard_map/pallas_call | solution.py:207
  14.7 1.3 %copy.7 = bf16[2,8,128]{2,1,0:T(8,128)(2,1)} copy(bf16[2,8,128]{2,1,0:T(8,128)(2,1)} %shard_map.46) | data formatting | bytes 8192
